TPU v7x, 32 devices: a whole 2x2x4 slice. The times are simulated.
32 devices in a mesh: section: 4 (over z), dp: 2 (over x), mp: 4 (over y, core).
Axes of the slice: x: 2, y: 2, z: 4, core: 2. Of those that a mesh axis runs over, the one named last changes fastest.
Arguments:
- entrance: bfloat16 [2, 2, 96, 4096], P('dp'), may hold values from -6 to 6
- lengths: int32 [2, 2], P('dp'), may hold values from 24 to 96
- positives: int32 [2], replicated, may hold values from 0 to 1, each once
- norm_gains: float32 [4, 4096], P('section'), may hold values from 0.5 to 1.5
- query_proj: bfloat16 [4, 4096, 2048], P('section', None, 'mp'), may hold values from -0.09375 to 0.09375
- key_proj: bfloat16 [4, 4096, 512], P('section', None, 'mp'), may hold values from -0.09375 to 0.09375
- value_proj: bfloat16 [4, 4096, 512], P('section', None, 'mp'), may hold values from -0.09375 to 0.09375
- out_proj: bfloat16 [4, 2048, 4096], P('section', 'mp'), may hold values from -0.125 to 0.125
Outputs:
- losses: float32 [4, 7], P('section')
- norm_gain_grad: float32 [4, 4096], P('section', ('dp', 'mp'))
- query_proj_grad: float32 [4, 4096, 2048], P('section', 'dp', 'mp')
- key_proj_grad: float32 [4, 4096, 512], P('section', 'dp', 'mp')
- value_proj_grad: float32 [4, 4096, 512], P('section', 'dp', 'mp')
- out_proj_grad: float32 [4, 2048, 4096], P('section', 'mp', 'dp')
Inputs may be any that keep to these rules, and one draw needn't show every extreme that they name: positives is a permutation of the pair indices. `lengths`: tokens at or past a sequence's length are padding.
All inputs are finite; a program needn't handle non-finite values.
Results may differ from a plain program's by a relative error of at most 0.039.
Values may be sent and summed in bfloat16 or wider, within the bound.
A program may use at most 128 MiB of HBM per device.

v0:
```python
import jax
import jax.numpy as jnp
from jax import lax
from jax.sharding import PartitionSpec as P

HEAD = 128
WIDTHS = 7
EPSILON = 1e-05
SOFTMAX_TEMPER = 0.05
ROPE_BASE = 500000.0


def passed_along(value, axis, steps):
    count = lax.axis_size(axis)
    first, last = (max(0, -steps), min(count, count - steps))
    return lax.ppermute(value, axis, [(source, source + steps) for source in range(first, last)])


def rope_tables(length, head_size):
    half_size = head_size // 2
    inverse_freq = ROPE_BASE ** (-jnp.arange(half_size, dtype=jnp.float32) * 2.0 / head_size)
    angles = jnp.arange(length, dtype=jnp.float32)[:, None] * inverse_freq[None, :]
    return (jnp.cos(angles), jnp.sin(angles))


def rotate(values, cosine, sine_table):
    half_size = values.shape[-1] // 2
    first_half = values[..., :half_size]
    second = values[..., half_size:]
    cosine = cosine[None, :, None, :]
    sine_table = sine_table[None, :, None, :]
    return jnp.concatenate(
        [first_half * cosine - second * sine_table, second * cosine + first_half * sine_table],
        axis=-1,
    )


def attend(query_pre, key_pre, value_pre):
    seq_count, length, query_width = query_pre.shape
    query_heads = query_width // HEAD
    kv_heads = key_pre.shape[-1] // HEAD
    group_size = query_heads // kv_heads
    cosine, sine_table = rope_tables(length, HEAD)
    query_vectors = rotate(
        query_pre.reshape(seq_count, length, query_heads, HEAD), cosine, sine_table
    ).astype(jnp.bfloat16)
    key_rows = rotate(
        key_pre.reshape(seq_count, length, kv_heads, HEAD), cosine, sine_table
    ).astype(jnp.bfloat16)
    values = value_pre.reshape(seq_count, length, kv_heads, HEAD).astype(jnp.bfloat16)
    query_vectors = query_vectors.reshape(seq_count, length, kv_heads, group_size, HEAD)
    scores = jnp.einsum(
        "sikge,sjke->skgij", query_vectors.astype(jnp.float32), key_rows.astype(jnp.float32)
    ) * HEAD ** (-0.5)
    causal = (
        jnp.arange(length, dtype=jnp.int32)[:, None] >= jnp.arange(length, dtype=jnp.int32)[None, :]
    )
    scores = jnp.where(causal, scores, -1e30)
    weights = jax.nn.softmax(scores, axis=-1).astype(jnp.bfloat16)
    mixture = jnp.einsum(
        "skgij,sjke->sikge", weights.astype(jnp.float32), values.astype(jnp.float32)
    )
    return mixture.reshape(seq_count, length, query_heads * HEAD)


def normalize(hidden_f, gain_vector):
    inv_rms = lax.rsqrt(jnp.mean(hidden_f * hidden_f, axis=-1, keepdims=True) + EPSILON)
    return hidden_f * inv_rms * gain_vector


def contract_rows(left, right):
    return lax.dot_general(
        left, right, (((0,), (0,)), ((), ())), preferred_element_type=jnp.float32
    )


def contract_last(left, right):
    return lax.dot_general(
        left, right, (((left.ndim - 1,), (1,)), ((), ())), preferred_element_type=jnp.float32
    )


def pool_exits(batch_rows, mask_of_valid, counts):
    total_value = jnp.einsum("ki,kiu->ku", mask_of_valid, batch_rows.astype(jnp.float32))
    return total_value / counts[:, None]


def spread_grad(exit_grad, mask_of_valid, counts):
    return mask_of_valid[:, :, None] * (exit_grad / counts[:, None])[:, None, :]


def matryoshka_losses(pooled, positives):
    pair_total = pooled.shape[0]
    target = (jnp.arange(pair_total, dtype=jnp.int32)[None, :] == positives[:, None]).astype(
        jnp.float32
    )
    losses = []
    for level_index in range(WIDTHS):
        leading_width = pooled.shape[-1] // 2**level_index
        query_vectors = pooled[:, 0, :leading_width]
        passage_rows = pooled[:, 1, :leading_width]
        query_vectors = query_vectors * lax.rsqrt(
            jnp.mean(query_vectors * query_vectors, axis=-1, keepdims=True) + 1e-06
        )
        passage_rows = passage_rows * lax.rsqrt(
            jnp.mean(passage_rows * passage_rows, axis=-1, keepdims=True) + 1e-06
        )
        score_matrix = jnp.dot(query_vectors, passage_rows.T, precision=lax.Precision.HIGHEST) / (
            leading_width * SOFTMAX_TEMPER
        )
        picked = jnp.sum(score_matrix * target, axis=-1)
        losses.append(jnp.mean(jax.nn.logsumexp(score_matrix, axis=-1) - picked))
    return jnp.stack(losses)


def pass_along(batch_rows, direction):
    return passed_along(batch_rows, "section", direction)


def forward_section(hidden, gain_vector, query_weight, key_weight, value_weight, out_weight):
    hidden_f = hidden.astype(jnp.float32)
    normed = normalize(hidden_f, gain_vector).astype(jnp.bfloat16)
    mixture = attend(
        jnp.dot(normed, query_weight, preferred_element_type=jnp.float32),
        jnp.dot(normed, key_weight, preferred_element_type=jnp.float32),
        jnp.dot(normed, value_weight, preferred_element_type=jnp.float32),
    ).astype(jnp.bfloat16)
    partial_value = jnp.dot(mixture, out_weight, preferred_element_type=jnp.float32)
    total_value = lax.psum(partial_value.astype(jnp.bfloat16), "mp").astype(jnp.float32)
    return (hidden_f + total_value).astype(jnp.bfloat16)


def backward_section(
    hidden, upstream, gain_vector, query_weight, key_weight, value_weight, out_weight
):
    hidden_f = hidden.astype(jnp.float32)
    inv_rms = lax.rsqrt(jnp.mean(hidden_f * hidden_f, axis=-1, keepdims=True) + EPSILON)
    normed = normalize(hidden_f, gain_vector).astype(jnp.bfloat16)
    out_grad = upstream.astype(jnp.bfloat16)
    mixture_f, pullback = jax.vjp(
        attend,
        jnp.dot(normed, query_weight, preferred_element_type=jnp.float32),
        jnp.dot(normed, key_weight, preferred_element_type=jnp.float32),
        jnp.dot(normed, value_weight, preferred_element_type=jnp.float32),
    )
    mixture = mixture_f.astype(jnp.bfloat16)
    mixture_grad = contract_last(out_grad, out_weight).astype(jnp.bfloat16)
    pulled = pullback(lax.optimization_barrier(mixture_grad).astype(jnp.float32))
    query_grad, key_grad, value_grad = [piece_grad.astype(jnp.bfloat16) for piece_grad in pulled]
    member_grad = (
        contract_last(query_grad, query_weight)
        + contract_last(key_grad, key_weight)
        + contract_last(value_grad, value_weight)
    )
    normed_grad = lax.psum(member_grad.astype(jnp.bfloat16), "mp").astype(jnp.float32)
    rounded = lax.optimization_barrier(member_grad.astype(jnp.bfloat16)).astype(jnp.float32)
    gain_term = jnp.sum(rounded * hidden_f * inv_rms, axis=(0, 1))
    _, norm_pull = jax.vjp(lambda values: normalize(values, gain_vector), hidden_f)
    input_grad = (upstream + norm_pull(normed_grad)[0]).astype(jnp.bfloat16)
    width_all = hidden.shape[-1]
    head_grads = jnp.concatenate([query_grad, key_grad, value_grad], axis=-1)
    stored_now = (
        normed.reshape(-1, width_all),
        out_grad.reshape(-1, width_all),
        head_grads.reshape(-1, head_grads.shape[-1]),
        mixture.reshape(-1, mixture.shape[-1]),
        gain_term,
    )
    return (input_grad, stored_now)


def local(entrance, lengths, positives, norm_gains, query_proj, key_proj, value_proj, out_proj):
    section_count = lax.axis_size("section")
    section_index = lax.axis_index("section")
    pair_count = entrance.shape[0]
    seq_count = 2 * pair_count
    length = entrance.shape[2]
    width_all = entrance.shape[3]
    start_hidden = entrance.reshape(seq_count, length, width_all)
    mask_of_valid = (
        jnp.arange(length, dtype=jnp.int32)[None, :] < lengths.reshape(seq_count, 1)
    ).astype(jnp.float32)
    counts = jnp.sum(mask_of_valid, axis=1)
    gain_vector = norm_gains[0]
    query_weight = query_proj[0]
    key_weight = key_proj[0]
    value_weight = value_proj[0]
    out_weight = out_proj[0]
    current = start_hidden
    saved_input = start_hidden
    exit_rows = start_hidden
    for section_turn in range(section_count):
        produced = forward_section(
            current, gain_vector, query_weight, key_weight, value_weight, out_weight
        )
        chosen = section_index == section_turn
        saved_input = jnp.where(chosen, current, saved_input)
        exit_rows = jnp.where(chosen, produced, exit_rows)
        if section_turn + 1 < section_count:
            arrived = pass_along(produced, 1)
            current = jnp.where(section_index == 0, start_hidden, arrived)
    pooled = pool_exits(exit_rows, mask_of_valid, counts).reshape(pair_count, 2, width_all)
    gathered = lax.all_gather(pooled.astype(jnp.bfloat16), "dp", axis=0, tiled=True).astype(
        pooled.dtype
    )
    losses_now, pullback = jax.vjp(
        lambda embedded: matryoshka_losses(embedded, positives), gathered
    )
    pair_grads = pullback(jnp.ones((WIDTHS,), jnp.float32))[0]
    own_losses = losses_now[None]
    own_grad = lax.dynamic_slice_in_dim(
        pair_grads, lax.axis_index("dp") * pair_count, pair_count, 0
    )
    token_grad = spread_grad(own_grad.reshape(seq_count, width_all), mask_of_valid, counts)
    incoming = jnp.zeros(start_hidden.shape, jnp.bfloat16)
    stored = None
    for section_turn in range(section_count):
        owner_section = section_count - 1 - section_turn
        upstream = token_grad + incoming.astype(jnp.float32)
        input_grad, stored_now = backward_section(
            saved_input, upstream, gain_vector, query_weight, key_weight, value_weight, out_weight
        )
        chosen = section_index == owner_section
        if stored is None:
            stored = stored_now
        else:
            stored = jax.tree.map(
                lambda fresh, former: jnp.where(chosen, fresh, former), stored_now, stored
            )
        if section_turn + 1 < section_count:
            incoming = pass_along(input_grad, -1)
    normed_rows, out_rows, head_grads, mixture_rows, gain_term = stored
    gain_share = lax.psum_scatter(gain_term, ("dp", "mp"), scatter_dimension=0, tiled=True)
    normed_cols, out_cols = (
        lax.all_to_all(normed_rows, "dp", split_axis=1, concat_axis=0, tiled=True),
        lax.all_to_all(out_rows, "dp", split_axis=1, concat_axis=0, tiled=True),
    )
    head_piece = lax.all_gather(head_grads, "dp", axis=0, tiled=True)
    mixture_piece = lax.all_gather(mixture_rows, "dp", axis=0, tiled=True)
    weight_sums = jnp.concatenate(
        [contract_rows(normed_cols, head_piece), contract_rows(out_cols, mixture_piece)], axis=1
    )
    query_cols = query_weight.shape[1]
    kv_cols = key_weight.shape[1]
    query_grad_out = weight_sums[:, :query_cols][None]
    key_grad_out = weight_sums[:, query_cols : query_cols + kv_cols][None]
    value_grad_out = weight_sums[:, query_cols + kv_cols : query_cols + 2 * kv_cols][None]
    out_grad_out = weight_sums[:, query_cols + 2 * kv_cols :].T[None]
    return (
        own_losses,
        gain_share[None],
        query_grad_out,
        key_grad_out,
        value_grad_out,
        out_grad_out,
    )


def solution(mesh):
    in_specs = (
        P("dp", None, None, None),
        P("dp", None),
        P(),
        P("section", None),
        P("section", None, "mp"),
        P("section", None, "mp"),
        P("section", None, "mp"),
        P("section", "mp", None),
    )
    out_specs = (
        P("section", None),
        P("section", ("dp", "mp")),
        P("section", "dp", "mp"),
        P("section", "dp", "mp"),
        P("section", "dp", "mp"),
        P("section", "mp", "dp"),
    )
    return jax.shard_map(local, mesh=mesh, in_specs=in_specs, out_specs=out_specs, check_vma=False)
```

profile of v0, /device:TPU:0, one launch (start us, length us, event | category | flops | bytes accessed | tf_op | source)
XLA Modules:
  0.0 794.6 jit_solution(6625503369172345784)
XLA Ops:
  9.4 6.4 copy.140
  23.3 4.3 convolution_convert_fusion.3
  27.7 45.7 %all-reduce.39.cloned.1.call-done = bf16[2,96,4096]{2,1,0:T(8,128)(2,1)} async-done(((bf16[2,96,4096]{2,1,0:T(8,128)(2,1)}), bf16[2,96,4096]{2,1,0:T(8,128)(2,1)}) %all-reduce.39.cloned.1.call-update) | async-done | bytes 1572880 | tf_op jit(solution)/shard_map/psum | solution.py:129
  76.5 4.5 collective-permute-start
  81.0 32.7 %collective-permute-done = bf16[2,96,4096]{2,1,0:T(8,128)(2,1)} collective-permute-done((bf16[2,96,4096]{2,1,0:T(8,128)(2,1)}, bf16[2,96,4096]{2,1,0:T(8,128)(2,1)}, u32[]{:S(2)}, u32[]{:S(2)}) %collective-permute-start) | collective-permute-done | bytes 1572896 | tf_op jit(solution)/shard_map/ppermute | solution.py:16
  120.0 4.3 convolution_convert_fusion.2
  124.4 45.4 %all-reduce.41.cloned.1.call-done = bf16[2,96,4096]{2,1,0:T(8,128)(2,1)} async-done(((bf16[2,96,4096]{2,1,0:T(8,128)(2,1)}), bf16[2,96,4096]{2,1,0:T(8,128)(2,1)}) %all-reduce.41.cloned.1.call-update) | async-done | bytes 1572880 | tf_op jit(solution)/shard_map/psum | solution.py:129
  172.2 3.9 collective-permute-start.1
  176.2 33.3 %collective-permute-done.1 = bf16[2,96,4096]{2,1,0:T(8,128)(2,1)S(1)} collective-permute-done((bf16[2,96,4096]{2,1,0:T(8,128)(2,1)S(1)}, bf16[2,96,4096]{2,1,0:T(8,128)(2,1)S(1)}, u32[]{:S(2)}, u32[]{:S(2)}) %collective-permute-start.1) | collective-permute-done | bytes 1572896 | tf_op jit(solution)/shard_map/ppermute | solution.py:16
  215.7 4.5 convolution_convert_fusion.1
  220.2 44.0 %all-reduce.43.cloned.1.call-done = bf16[2,96,4096]{2,1,0:T(8,128)(2,1)} async-done(((bf16[2,96,4096]{2,1,0:T(8,128)(2,1)}), bf16[2,96,4096]{2,1,0:T(8,128)(2,1)}) %all-reduce.43.cloned.1.call-update) | async-done | bytes 1572880 | tf_op jit(solution)/shard_map/psum | solution.py:129
  267.4 4.5 collective-permute-start.2
  273.3 31.3 %collective-permute-done.2 = bf16[2,96,4096]{2,1,0:T(8,128)(2,1)} collective-permute-done((bf16[2,96,4096]{2,1,0:T(8,128)(2,1)}, bf16[2,96,4096]{2,1,0:T(8,128)(2,1)}, u32[]{:S(2)}, u32[]{:S(2)}) %collective-permute-start.2) | collective-permute-done | bytes 1572896 | tf_op jit(solution)/shard_map/ppermute | solution.py:16
  319.5 4.4 convolution_convert_fusion
  326.7 41.8 %all-reduce.45.cloned.1.call-done = bf16[2,96,4096]{2,1,0:T(8,128)(2,1)} async-done(((bf16[2,96,4096]{2,1,0:T(8,128)(2,1)}), bf16[2,96,4096]{2,1,0:T(8,128)(2,1)}) %all-reduce.45.cloned.1.call-update) | async-done | bytes 1572880 | tf_op jit(solution)/shard_map/psum | solution.py:129
  368.5 4.4 fusion.65
  373.0 4.6 all-gather.1
  402.4 43.0 %all-reduce.47.cloned.1.call-done = bf16[2,96,4096]{2,1,0:T(8,128)(2,1)} async-done(((bf16[2,96,4096]{2,1,0:T(8,128)(2,1)}), bf16[2,96,4096]{2,1,0:T(8,128)(2,1)}) %all-reduce.47.cloned.1.call-update) | async-done | bytes 1572880 | tf_op jit(solution)/shard_map/psum | solution.py:155
  451.2 36.2 %collective-permute-done.3 = bf16[2,96,4096]{2,1,0:T(8,128)(2,1)S(1)} collective-permute-done((bf16[2,96,4096]{2,1,0:T(8,128)(2,1)S(1)}, bf16[2,96,4096]{2,1,0:T(8,128)(2,1)S(1)}, u32[]{:S(2)}, u32[]{:S(2)}) %collective-permute-start.3) | collective-permute-done | bytes 1572896 | tf_op jit(solution)/shard_map/ppermute | solution.py:16
  503.0 42.1 %all-reduce.49.cloned.1.call-done = bf16[2,96,4096]{2,1,0:T(8,128)(2,1)} async-done(((bf16[2,96,4096]{2,1,0:T(8,128)(2,1)}), bf16[2,96,4096]{2,1,0:T(8,128)(2,1)}) %all-reduce.49.cloned.1.call-update) | async-done | bytes 1572880 | tf_op jit(solution)/shard_map/psum | solution.py:155
  550.4 36.4 %collective-permute-done.4 = bf16[2,96,4096]{2,1,0:T(8,128)(2,1)S(1)} collective-permute-done((bf16[2,96,4096]{2,1,0:T(8,128)(2,1)S(1)}, bf16[2,96,4096]{2,1,0:T(8,128)(2,1)S(1)}, u32[]{:S(2)}, u32[]{:S(2)}) %collective-permute-start.4) | collective-permute-done | bytes 1572896 | tf_op jit(solution)/shard_map/ppermute | solution.py:16
  602.5 42.2 %all-reduce.51.cloned.1.call-done = bf16[2,96,4096]{2,1,0:T(8,128)(2,1)} async-done(((bf16[2,96,4096]{2,1,0:T(8,128)(2,1)}), bf16[2,96,4096]{2,1,0:T(8,128)(2,1)}) %all-reduce.51.cloned.1.call-update) | async-done | bytes 1572880 | tf_op jit(solution)/shard_map/psum | solution.py:155
  661.1 4.6 all-to-all-start
  676.2 5.6 mul.2560
  682.4 9.3 %all_gather.11 = bf16[384,512]{1,0:T(8,128)(2,1)} all-gather(bf16[192,512]{1,0:T(8,128)(2,1)} %bitcast.1023), channel_id=1, replica_groups=mesh['section'=4,'dp'=2,'mp'=4] {'dp'}, dimensions={0}, use_global_device_ids=true | all-gather | bytes 589824 | tf_op jit(solution)/shard_map/all_gather | solution.py:239
  708.2 3.9 reshape.1123
  723.2 8.6 %all_gather.10 = bf16[384,768]{1,0:T(8,128)(2,1)S(1)} all-gather(bf16[192,768]{1,0:T(8,128)(2,1)S(1)} %maximum_select_fusion), channel_id=1, replica_groups=mesh['section'=4,'dp'=2,'mp'=4] {'dp'}, dimensions={0}, use_global_device_ids=true | all-gather | bytes 884736 | tf_op jit(solution)/shard_map/all_gather | solution.py:238
  731.8 5.4 fusion.63
  737.1 4.9 all-to-all-start.1
  752.7 24.6 %all-reduce.30 = f32[4096]{0:T(1024)S(1)} all-reduce(f32[4096]{0:T(1024)S(1)} %select_select_fusion), channel_id=3, replica_groups=mesh['section'=4,'dp'=2,'mp'=4] {'dp','mp'}, use_global_device_ids=true, to_apply=%region_90.91.clone | all-reduce | flops 4096 | bytes 32768
  777.9 4.7 slice_bitcast_fusion
  782.6 4.7 convolution_bitcast_fusion
  (488 shorter events, 176.6 us)
Async XLA Ops:
  7.2 66.2 %all-reduce.39.cloned.1.call-start = ((), (), s32[]{:S(2)}) async-start(), calls=%async_computation.2 | async-start | bytes 3145728 | tf_op jit(solution)/shard_map/psum | solution.py:129
  7.3 317.0 %copy-start.62 = (pred[96,96]{0,1:T(8,128)(4,1)}, pred[96,96]{0,1:T(8,128)(4,1)S(1)}, u32[]{:S(2)}) copy-start(pred[96,96]{0,1:T(8,128)(4,1)S(1)} %iota_compare_fusion) | copy-start | bytes 27652
  27.6 142.1 %all-reduce.41.cloned.1.call-start = ((), (), s32[]{:S(2)}) async-start(), calls=%async_computation.3 | async-start | bytes 3145728 | tf_op jit(solution)/shard_map/psum | solution.py:129
  76.5 37.2 %collective-permute-start = (bf16[2,96,4096]{2,1,0:T(8,128)(2,1)}, bf16[2,96,4096]{2,1,0:T(8,128)(2,1)}, u32[]{:S(2)}, u32[]{:S(2)}) collective-permute-start(bf16[2,96,4096]{2,1,0:T(8,128)(2,1)} %fusion.25), channel_id=1, source_target_pairs={{0,8},{8,16},{16,24},{1,9},{9,17},{17,25},{2,10},{10,18},{18,26},{... | collective-permute-start | bytes 4718600 | tf_op jit(solution)/shard_map/ppermute | solution.py:16
  81.0 33.4 %copy-start.11 = (bf16[1,4096,128]{2,1,0:T(8,128)(2,1)S(1)}, bf16[1,4096,128]{2,1,0:T(8,128)(2,1)}, u32[]{:S(2)}) copy-start(bf16[1,4096,128]{2,1,0:T(8,128)(2,1)} %param.13) | copy-start | bytes 3145732
  81.0 34.2 %copy-start.41 = (bf16[512,4096]{1,0:T(8,128)(2,1)S(1)}, bf16[512,4096]{1,0:T(8,128)(2,1)}, u32[]{:S(2)}) copy-start(bf16[512,4096]{1,0:T(8,128)(2,1)} %copy.140) | copy-start | bytes 12582916
  124.3 140.0 %all-reduce.43.cloned.1.call-start = ((), (), s32[]{:S(2)}) async-start(), calls=%async_computation.4 | async-start | bytes 3145728 | tf_op jit(solution)/shard_map/psum | solution.py:129
  172.2 38.0 %copy-start.52 = (bf16[2,96,4096]{2,1,0:T(8,128)(2,1)}, bf16[2,96,4096]{2,1,0:T(8,128)(2,1)S(1)}, u32[]{:S(2)}) copy-start(bf16[2,96,4096]{2,1,0:T(8,128)(2,1)S(1)} %fusion.29) | copy-start | bytes 4718596
  172.2 38.0 %copy-start.12 = (bf16[1,4096,128]{2,1,0:T(8,128)(2,1)S(1)}, bf16[1,4096,128]{2,1,0:T(8,128)(2,1)}, u32[]{:S(2)}) copy-start(bf16[1,4096,128]{2,1,0:T(8,128)(2,1)} %param.13) | copy-start | bytes 3145732
  172.2 38.7 %copy-start.42 = (bf16[512,4096]{1,0:T(8,128)(2,1)S(1)}, bf16[512,4096]{1,0:T(8,128)(2,1)}, u32[]{:S(2)}) copy-start(bf16[512,4096]{1,0:T(8,128)(2,1)} %copy.140) | copy-start | bytes 12582916
  172.2 37.2 %collective-permute-start.1 = (bf16[2,96,4096]{2,1,0:T(8,128)(2,1)S(1)}, bf16[2,96,4096]{2,1,0:T(8,128)(2,1)S(1)}, u32[]{:S(2)}, u32[]{:S(2)}) collective-permute-start(bf16[2,96,4096]{2,1,0:T(8,128)(2,1)S(1)} %fusion.29), channel_id=1, source_target_pairs={{0,8},{8,16},{16,24},{1,9},{9,17},{17,25},{2,10},{10,18},{18,26},{... | collective-permute-start | bytes 4718600 | tf_op jit(solution)/shard_map/ppermute | solution.py:16
  215.7 48.6 %copy-start.24 = (bf16[2,96,4096]{2,1,0:T(8,128)(2,1)S(1)}, bf16[2,96,4096]{2,1,0:T(8,128)(2,1)}, u32[]{:S(2)}) copy-start(bf16[2,96,4096]{2,1,0:T(8,128)(2,1)} %copy-done.23) | copy-start | bytes 4718596
  220.2 51.8 %copy-start.114 = (s32[1,2]{1,0:T(1,128)S(1)}, s32[1,2]{1,0:T(1,128)}, u32[]{:S(2)}) copy-start(s32[1,2]{1,0:T(1,128)} %param.9) | copy-start | bytes 28
  220.2 148.3 %all-reduce.45.cloned.1.call-start = ((), (), s32[]{:S(2)}) async-start(), calls=%async_computation.5 | async-start | bytes 3145728 | tf_op jit(solution)/shard_map/psum | solution.py:129
  267.4 37.2 %collective-permute-start.2 = (bf16[2,96,4096]{2,1,0:T(8,128)(2,1)}, bf16[2,96,4096]{2,1,0:T(8,128)(2,1)}, u32[]{:S(2)}, u32[]{:S(2)}) collective-permute-start(bf16[2,96,4096]{2,1,0:T(8,128)(2,1)} %fusion.33), channel_id=1, source_target_pairs={{0,8},{8,16},{16,24},{1,9},{9,17},{17,25},{2,10},{10,18},{18,26},{... | collective-permute-start | bytes 4718600 | tf_op jit(solution)/shard_map/ppermute | solution.py:16
  323.9 121.5 %all-reduce.47.cloned.1.call-start = ((), (), s32[]{:S(2)}) async-start(), calls=%async_computation.6 | async-start | bytes 3145728 | tf_op jit(solution)/shard_map/psum | solution.py:155
  324.3 71.7 %copy-start.60 = (bf16[2,96,4,128]{3,1,2,0:T(8,128)(2,1)}, bf16[2,96,4,128]{3,1,2,0:T(8,128)(2,1)S(1)}, u32[]{:S(2)}) copy-start(bf16[2,96,4,128]{3,1,2,0:T(8,128)(2,1)S(1)} %pad_maximum_fusion) | copy-start | bytes 589828
  324.6 71.7 %copy-start.88 = (f32[2,4,96]{2,1,0:T(4,128)}, f32[2,4,96]{2,1,0:T(4,128)S(1)}, u32[]{:S(2)}) copy-start(f32[2,4,96]{2,1,0:T(4,128)S(1)} %get-tuple-element.178) | copy-start | bytes 9220
  324.7 71.6 %copy-start.103 = (f32[2,4,96]{2,1,0:T(4,128)}, f32[2,4,96]{2,1,0:T(4,128)S(1)}, u32[]{:S(2)}) copy-start(f32[2,4,96]{2,1,0:T(4,128)S(1)} %fusion.513) | copy-start | bytes 9220
  324.7 69.9 %copy-start.92 = (f32[2,4,96]{2,1,0:T(4,128)}, f32[2,4,96]{2,1,0:T(4,128)S(1)}, u32[]{:S(2)}) copy-start(f32[2,4,96]{2,1,0:T(4,128)S(1)} %multiply_divide_fusion) | copy-start | bytes 9220
  326.7 68.0 %copy-start.53 = (bf16[2,96,128,1]{2,1,3,0:T(8,128)(2,1)}, bf16[2,96,128,1]{2,1,3,0:T(8,128)(2,1)S(1)}, u32[]{:S(2)}) copy-start(bf16[2,96,128,1]{2,1,3,0:T(8,128)(2,1)S(1)} %fusion.144) | copy-start | bytes 147460
  368.5 22.3 %copy-start.5 = (bf16[1,512,4096]{2,1,0:T(8,128)(2,1)S(1)}, bf16[1,512,4096]{2,1,0:T(8,128)(2,1)}, u32[]{:S(2)}) copy-start(bf16[1,512,4096]{2,1,0:T(8,128)(2,1)} %param.15) | copy-start | bytes 12582916
  372.9 17.9 %copy-start.93 = (f32[2,96]{1,0:T(2,128)S(1)}, f32[2,96]{1,0:T(2,128)}, u32[]{:S(2)}) copy-start(f32[2,96]{1,0:T(2,128)} %get-tuple-element.119) | copy-start | bytes 2308
  402.4 142.8 %all-reduce.49.cloned.1.call-start = ((), (), s32[]{:S(2)}) async-start(), calls=%async_computation.7 | async-start | bytes 3145728 | tf_op jit(solution)/shard_map/psum | solution.py:155
  448.1 42.0 %copy-start.6 = (bf16[1,512,4096]{2,1,0:T(8,128)(2,1)S(1)}, bf16[1,512,4096]{2,1,0:T(8,128)(2,1)}, u32[]{:S(2)}) copy-start(bf16[1,512,4096]{2,1,0:T(8,128)(2,1)} %param.15) | copy-start | bytes 12582916
  449.4 38.0 %collective-permute-start.3 = (bf16[2,96,4096]{2,1,0:T(8,128)(2,1)S(1)}, bf16[2,96,4096]{2,1,0:T(8,128)(2,1)S(1)}, u32[]{:S(2)}, u32[]{:S(2)}) collective-permute-start(bf16[2,96,4096]{2,1,0:T(8,128)(2,1)S(1)} %fusion.42), channel_id=1, source_target_pairs={{8,0},{16,8},{24,16},{9,1},{17,9},{25,17},{10,2},{18,10},{26,18},{... | collective-permute-start | bytes 4718600 | tf_op jit(solution)/shard_map/ppermute | solution.py:16
  503.0 141.7 %all-reduce.51.cloned.1.call-start = ((), (), s32[]{:S(2)}) async-start(), calls=%async_computation.8 | async-start | bytes 3145728 | tf_op jit(solution)/shard_map/psum | solution.py:155
  547.5 42.2 %copy-start.7 = (bf16[1,512,4096]{2,1,0:T(8,128)(2,1)S(1)}, bf16[1,512,4096]{2,1,0:T(8,128)(2,1)}, u32[]{:S(2)}) copy-start(bf16[1,512,4096]{2,1,0:T(8,128)(2,1)} %param.15) | copy-start | bytes 12582916
  548.9 37.9 %collective-permute-start.4 = (bf16[2,96,4096]{2,1,0:T(8,128)(2,1)S(1)}, bf16[2,96,4096]{2,1,0:T(8,128)(2,1)S(1)}, u32[]{:S(2)}, u32[]{:S(2)}) collective-permute-start(bf16[2,96,4096]{2,1,0:T(8,128)(2,1)S(1)} %fusion.39), channel_id=1, source_target_pairs={{8,0},{16,8},{24,16},{9,1},{17,9},{25,17},{10,2},{18,10},{26,18},{... | collective-permute-start | bytes 4718600 | tf_op jit(solution)/shard_map/ppermute | solution.py:16
  649.6 53.3 %collective-permute-start.5 = (bf16[2,96,4096]{2,1,0:T(8,128)(2,1)}, bf16[2,96,4096]{2,1,0:T(8,128)(2,1)}, u32[]{:S(2)}, u32[]{:S(2)}) collective-permute-start(bf16[2,96,4096]{2,1,0:T(8,128)(2,1)} %fusion.41), channel_id=1, source_target_pairs={{8,0},{16,8},{24,16},{9,1},{17,9},{25,17},{10,2},{18,10},{26,18},{... | collective-permute-start | bytes 4718600 | tf_op jit(solution)/shard_map/ppermute | solution.py:16
  661.1 76.0 %all-to-all-start = ((bf16[192,2,2048]{2,0,1:T(8,128)(2,1)}), bf16[192,2,2048]{2,0,1:T(8,128)(2,1)}, u32[]{:S(2)}, u32[]{:S(2)}) async-start(bf16[192,2,2048]{2,0,1:T(8,128)(2,1)} %copy.95), calls=%async_computation | async-start | bytes 3145728 | tf_op jit(solution)/shard_map/all_to_all | solution.py:235
  737.1 45.5 %all-to-all-start.1 = ((bf16[192,2,2048]{2,0,1:T(8,128)(2,1)}), bf16[192,2,2048]{2,0,1:T(8,128)(2,1)}, u32[]{:S(2)}, u32[]{:S(2)}) async-start(bf16[192,2,2048]{2,0,1:T(8,128)(2,1)} %fusion.63), calls=%async_computation.1 | async-start | bytes 3145728 | tf_op jit(solution)/shard_map/all_to_all | solution.py:236
  (98 other events, 377.3 us)
Sparse Core Ops, SparseCore 0:
  27.8 45.5 all-reduce.38
  124.4 45.3 all-reduce.40
  220.3 43.9 all-reduce.42
  324.1 44.3 all-reduce.44
  402.5 42.9 all-reduce.46
  503.1 41.9 all-reduce.48
  602.6 41.9 all-reduce.50
where the time goes:
time: 805 us; the launch traced here: 795 us
  waiting for transfers between devices  474 us (59%)
  matrix products  102 us (13%)
  local copies, waits for them, and re-layouts  66.7 us (8%)
  other arithmetic  55.3 us (7%)
  blocking collectives  47.1 us (6%)
  starting transfers between devices  27.3 us (3%)
  between operations  21.9 us (3%)
    psum x4, waiting for transfers between devices, forward_section(): lax.psum(partial_value.astype(jnp.bfloat16), 'mp').astype(jnp.float32)  177 us
    ppermute x6, waiting for transfers between devices, passed_along(): lax.ppermute(value, axis, [(source, source + steps) for source in range(f...  170 us
    psum x3, waiting for transfers between devices, backward_section(): lax.psum(member_grad.astype(jnp.bfloat16), 'mp').astype(jnp.float32)  127 us
    unnamed x1, blocking collectives  24.6 us
    dot_general x16, matrix products, contract_last(): lax.dot_general(left, right, (((left.ndim - 1,), (1,)), ((), ())), prefer...  24.5 us
    unnamed x237, local copies, waits for them, and re-layouts  18.1 us
    dot_general x13, matrix products, attend(): jnp.einsum('skgij,sjke->sikge', weights.astype(jnp.float32), values.astyp...  17.9 us
    ppermute x6, starting transfers between devices, passed_along(): lax.ppermute(value, axis, [(source, source + steps) for source in range(f...  17.6 us
  transfers between devices with their start and end apart: 15, of which 12 were waited for; matrix products, arithmetic and copies ran while one was open for 9% of the time, Pallas kernels for 0%

commit v1 on v0

--- a/solution.py
+++ b/solution.py
@@ -152,7 +152,9 @@
         + contract_last(key_grad, key_weight)
         + contract_last(value_grad, value_weight)
     )
-    normed_grad = lax.psum(member_grad.astype(jnp.bfloat16), "mp").astype(jnp.float32)
+    normed_grad = jnp.sum(lax.all_gather(member_grad.astype(jnp.bfloat16), "mp"), axis=0).astype(
+        jnp.float32
+    )
     rounded = lax.optimization_barrier(member_grad.astype(jnp.bfloat16)).astype(jnp.float32)
     gain_term = jnp.sum(rounded * hidden_f * inv_rms, axis=(0, 1))
     _, norm_pull = jax.vjp(lambda values: normalize(values, gain_vector), hidden_f)

time: 805 us -> 835 us (1.037)
  other arithmetic: 55.3 us -> 72 us
  waiting for transfers between devices: 474 us -> 486 us
    all_gather x0 -> x3, waiting for transfers between devices: none -> 138 us  [backward_section(): lax.all_gather(member_grad.astype(jnp.bfloat16), 'mp')]
    psum x3 -> x0, waiting for transfers between devices: 127 us -> none  [backward_section(): lax.psum(member_grad.astype(jnp.bfloat16), 'mp').astype(jnp.float32)]
    reduce_sum x0 -> x3, other arithmetic: none -> 16.7 us  [backward_section(): jnp.sum(lax.all_gather(member_grad.astype(jnp.bfloat16), 'mp'), axis=0)]
  transfers between devices with their start and end apart: 15 -> 15, of which waited for: 12 -> 12; matrix products, arithmetic and copies ran while one was open for 9% -> 8% of each run, Pallas kernels for 0% -> 0%
where the time goes in v1:
time: 835 us; the launch traced here: 824 us
  waiting for transfers between devices  486 us (58%)
  matrix products  102 us (12%)
  other arithmetic  72 us (9%)
  local copies, waits for them, and re-layouts  66.7 us (8%)
  blocking collectives  49.1 us (6%)
  starting transfers between devices  27.1 us (3%)
  between operations  21.6 us (3%)
    psum x4, waiting for transfers between devices, forward_section(): lax.psum(partial_value.astype(jnp.bfloat16), 'mp').astype(jnp.float32)  177 us
    ppermute x6, waiting for transfers between devices, passed_along(): lax.ppermute(value, axis, [(source, source + steps) for source in range(f...  171 us
    all_gather x3, waiting for transfers between devices, backward_section(): lax.all_gather(member_grad.astype(jnp.bfloat16), 'mp')  138 us
    unnamed x1, blocking collectives  25.1 us
    dot_general x16, matrix products, contract_last(): lax.dot_general(left, right, (((left.ndim - 1,), (1,)), ((), ())), prefer...  24.5 us
    unnamed x237, local copies, waits for them, and re-layouts  18.1 us
    dot_general x13, matrix products, attend(): jnp.einsum('skgij,sjke->sikge', weights.astype(jnp.float32), values.astyp...  17.9 us
    dot_general x4, matrix products, forward_section(): jnp.dot(mixture, out_weight, preferred_element_type=jnp.float32)  17.5 us
  transfers between devices with their start and end apart: 15, of which 12 were waited for; matrix products, arithmetic and copies ran while one was open for 8% of the time, Pallas kernels for 0%

profile of v1, /device:TPU:0, one launch (start us, length us, event | category | flops | bytes accessed | tf_op | source)
XLA Modules:
  0.0 824.3 jit_solution(13228710092608984793)
XLA Ops:
  9.4 6.4 copy.140
  23.3 4.3 convolution_convert_fusion.3
  27.7 45.7 %all-reduce.36.cloned.1.call-done = bf16[2,96,4096]{2,1,0:T(8,128)(2,1)} async-done(((bf16[2,96,4096]{2,1,0:T(8,128)(2,1)}), bf16[2,96,4096]{2,1,0:T(8,128)(2,1)}) %all-reduce.36.cloned.1.call-update) | async-done | bytes 1572880 | tf_op jit(solution)/shard_map/psum | solution.py:129
  76.5 4.5 collective-permute-start
  81.0 32.7 %collective-permute-done = bf16[2,96,4096]{2,1,0:T(8,128)(2,1)} collective-permute-done((bf16[2,96,4096]{2,1,0:T(8,128)(2,1)}, bf16[2,96,4096]{2,1,0:T(8,128)(2,1)}, u32[]{:S(2)}, u32[]{:S(2)}) %collective-permute-start) | collective-permute-done | bytes 1572896 | tf_op jit(solution)/shard_map/ppermute | solution.py:16
  124.4 45.4 %all-reduce.38.cloned.1.call-done = bf16[2,96,4096]{2,1,0:T(8,128)(2,1)} async-done(((bf16[2,96,4096]{2,1,0:T(8,128)(2,1)}), bf16[2,96,4096]{2,1,0:T(8,128)(2,1)}) %all-reduce.38.cloned.1.call-update) | async-done | bytes 1572880 | tf_op jit(solution)/shard_map/psum | solution.py:129
  176.2 33.2 %collective-permute-done.1 = bf16[2,96,4096]{2,1,0:T(8,128)(2,1)S(1)} collective-permute-done((bf16[2,96,4096]{2,1,0:T(8,128)(2,1)S(1)}, bf16[2,96,4096]{2,1,0:T(8,128)(2,1)S(1)}, u32[]{:S(2)}, u32[]{:S(2)}) %collective-permute-start.1) | collective-permute-done | bytes 1572896 | tf_op jit(solution)/shard_map/ppermute | solution.py:16
  215.7 4.4 convolution_convert_fusion.1
  220.2 44.0 %all-reduce.40.cloned.1.call-done = bf16[2,96,4096]{2,1,0:T(8,128)(2,1)} async-done(((bf16[2,96,4096]{2,1,0:T(8,128)(2,1)}), bf16[2,96,4096]{2,1,0:T(8,128)(2,1)}) %all-reduce.40.cloned.1.call-update) | async-done | bytes 1572880 | tf_op jit(solution)/shard_map/psum | solution.py:129
  267.3 4.5 collective-permute-start.2
  273.2 31.3 %collective-permute-done.2 = bf16[2,96,4096]{2,1,0:T(8,128)(2,1)} collective-permute-done((bf16[2,96,4096]{2,1,0:T(8,128)(2,1)}, bf16[2,96,4096]{2,1,0:T(8,128)(2,1)}, u32[]{:S(2)}, u32[]{:S(2)}) %collective-permute-start.2) | collective-permute-done | bytes 1572896 | tf_op jit(solution)/shard_map/ppermute | solution.py:16
  319.5 4.4 convolution_convert_fusion
  326.6 41.8 %all-reduce.42.cloned.1.call-done = bf16[2,96,4096]{2,1,0:T(8,128)(2,1)} async-done(((bf16[2,96,4096]{2,1,0:T(8,128)(2,1)}), bf16[2,96,4096]{2,1,0:T(8,128)(2,1)}) %all-reduce.42.cloned.1.call-update) | async-done | bytes 1572880 | tf_op jit(solution)/shard_map/psum | solution.py:129
  368.4 4.4 fusion.65
  372.9 4.8 all-gather.4
  402.5 46.5 %all-gather.9.cloned.1.call-done = bf16[8,96,4096]{2,1,0:T(8,128)(2,1)} async-done(((bf16[2,96,4096]{2,1,0:T(8,128)(2,1)}), bf16[8,96,4096]{2,1,0:T(8,128)(2,1)}) %all-gather.9.cloned.1.call-update) | async-done | bytes 6291472 | tf_op jit(solution)/shard_map/all_gather | solution.py:155
  449.0 5.6 reduce_sum.872
  460.1 37.0 %collective-permute-done.3 = bf16[2,96,4096]{2,1,0:T(8,128)(2,1)S(1)} collective-permute-done((bf16[2,96,4096]{2,1,0:T(8,128)(2,1)S(1)}, bf16[2,96,4096]{2,1,0:T(8,128)(2,1)S(1)}, u32[]{:S(2)}, u32[]{:S(2)}) %collective-permute-start.3) | collective-permute-done | bytes 1572896 | tf_op jit(solution)/shard_map/ppermute | solution.py:16
  512.8 45.5 %all-gather.11.cloned.1.call-done = bf16[8,96,4096]{2,1,0:T(8,128)(2,1)} async-done(((bf16[2,96,4096]{2,1,0:T(8,128)(2,1)}), bf16[8,96,4096]{2,1,0:T(8,128)(2,1)}) %all-gather.11.cloned.1.call-update) | async-done | bytes 6291472 | tf_op jit(solution)/shard_map/all_gather | solution.py:155
  558.4 5.6 reduce_sum.875
  569.2 36.9 %collective-permute-done.4 = bf16[2,96,4096]{2,1,0:T(8,128)(2,1)S(1)} collective-permute-done((bf16[2,96,4096]{2,1,0:T(8,128)(2,1)S(1)}, bf16[2,96,4096]{2,1,0:T(8,128)(2,1)S(1)}, u32[]{:S(2)}, u32[]{:S(2)}) %collective-permute-start.4) | collective-permute-done | bytes 1572896 | tf_op jit(solution)/shard_map/ppermute | solution.py:16
  621.8 45.6 %all-gather.13.cloned.1.call-done = bf16[8,96,4096]{2,1,0:T(8,128)(2,1)} async-done(((bf16[2,96,4096]{2,1,0:T(8,128)(2,1)}), bf16[8,96,4096]{2,1,0:T(8,128)(2,1)}) %all-gather.13.cloned.1.call-update) | async-done | bytes 6291472 | tf_op jit(solution)/shard_map/all_gather | solution.py:155
  667.4 5.6 reduce_sum.878
  689.4 4.6 all-to-all-start
  704.5 5.6 mul.2560
  710.7 10.0 %all_gather.35 = bf16[384,512]{1,0:T(8,128)(2,1)} all-gather(bf16[192,512]{1,0:T(8,128)(2,1)} %bitcast.1029), channel_id=1, replica_groups=mesh['section'=4,'dp'=2,'mp'=4] {'dp'}, dimensions={0}, use_global_device_ids=true | all-gather | bytes 589824 | tf_op jit(solution)/shard_map/all_gather | solution.py:241
  752.2 9.1 %all_gather.34 = bf16[384,768]{1,0:T(8,128)(2,1)S(1)} all-gather(bf16[192,768]{1,0:T(8,128)(2,1)S(1)} %maximum_select_fusion), channel_id=1, replica_groups=mesh['section'=4,'dp'=2,'mp'=4] {'dp'}, dimensions={0}, use_global_device_ids=true | all-gather | bytes 884736 | tf_op jit(solution)/shard_map/all_gather | solution.py:240
  761.3 5.4 fusion.63
  766.7 4.8 all-to-all-start.1
  782.1 25.1 %all-reduce.30 = f32[4096]{0:T(1024)S(1)} all-reduce(f32[4096]{0:T(1024)S(1)} %select_select_fusion), channel_id=6, replica_groups=mesh['section'=4,'dp'=2,'mp'=4] {'dp','mp'}, use_global_device_ids=true, to_apply=%region_90.91.clone | all-reduce | flops 4096 | bytes 32768
  807.9 4.7 slice_bitcast_fusion
  812.6 4.7 convolution_bitcast_fusion
  (491 shorter events, 188.5 us)
Async XLA Ops:
  7.2 66.2 %all-reduce.36.cloned.1.call-start = ((), (), s32[]{:S(2)}) async-start(), calls=%async_computation.2 | async-start | bytes 3145728 | tf_op jit(solution)/shard_map/psum | solution.py:129
  7.3 316.9 %copy-start.62 = (pred[96,96]{0,1:T(8,128)(4,1)}, pred[96,96]{0,1:T(8,128)(4,1)S(1)}, u32[]{:S(2)}) copy-start(pred[96,96]{0,1:T(8,128)(4,1)S(1)} %iota_compare_fusion) | copy-start | bytes 27652
  27.6 142.1 %all-reduce.38.cloned.1.call-start = ((), (), s32[]{:S(2)}) async-start(), calls=%async_computation.3 | async-start | bytes 3145728 | tf_op jit(solution)/shard_map/psum | solution.py:129
  76.5 37.2 %collective-permute-start = (bf16[2,96,4096]{2,1,0:T(8,128)(2,1)}, bf16[2,96,4096]{2,1,0:T(8,128)(2,1)}, u32[]{:S(2)}, u32[]{:S(2)}) collective-permute-start(bf16[2,96,4096]{2,1,0:T(8,128)(2,1)} %fusion.25), channel_id=1, source_target_pairs={{0,8},{8,16},{16,24},{1,9},{9,17},{17,25},{2,10},{10,18},{18,26},{... | collective-permute-start | bytes 4718600 | tf_op jit(solution)/shard_map/ppermute | solution.py:16
  81.0 33.4 %copy-start.11 = (bf16[1,4096,128]{2,1,0:T(8,128)(2,1)S(1)}, bf16[1,4096,128]{2,1,0:T(8,128)(2,1)}, u32[]{:S(2)}) copy-start(bf16[1,4096,128]{2,1,0:T(8,128)(2,1)} %param.13) | copy-start | bytes 3145732
  81.0 34.2 %copy-start.41 = (bf16[512,4096]{1,0:T(8,128)(2,1)S(1)}, bf16[512,4096]{1,0:T(8,128)(2,1)}, u32[]{:S(2)}) copy-start(bf16[512,4096]{1,0:T(8,128)(2,1)} %copy.140) | copy-start | bytes 12582916
  124.3 139.9 %all-reduce.40.cloned.1.call-start = ((), (), s32[]{:S(2)}) async-start(), calls=%async_computation.4 | async-start | bytes 3145728 | tf_op jit(solution)/shard_map/psum | solution.py:129
  172.2 38.0 %copy-start.52 = (bf16[2,96,4096]{2,1,0:T(8,128)(2,1)}, bf16[2,96,4096]{2,1,0:T(8,128)(2,1)S(1)}, u32[]{:S(2)}) copy-start(bf16[2,96,4096]{2,1,0:T(8,128)(2,1)S(1)} %fusion.29) | copy-start | bytes 4718596
  172.2 38.0 %copy-start.12 = (bf16[1,4096,128]{2,1,0:T(8,128)(2,1)S(1)}, bf16[1,4096,128]{2,1,0:T(8,128)(2,1)}, u32[]{:S(2)}) copy-start(bf16[1,4096,128]{2,1,0:T(8,128)(2,1)} %param.13) | copy-start | bytes 3145732
  172.2 38.7 %copy-start.42 = (bf16[512,4096]{1,0:T(8,128)(2,1)S(1)}, bf16[512,4096]{1,0:T(8,128)(2,1)}, u32[]{:S(2)}) copy-start(bf16[512,4096]{1,0:T(8,128)(2,1)} %copy.140) | copy-start | bytes 12582916
  172.2 37.2 %collective-permute-start.1 = (bf16[2,96,4096]{2,1,0:T(8,128)(2,1)S(1)}, bf16[2,96,4096]{2,1,0:T(8,128)(2,1)S(1)}, u32[]{:S(2)}, u32[]{:S(2)}) collective-permute-start(bf16[2,96,4096]{2,1,0:T(8,128)(2,1)S(1)} %fusion.29), channel_id=1, source_target_pairs={{0,8},{8,16},{16,24},{1,9},{9,17},{17,25},{2,10},{10,18},{18,26},{... | collective-permute-start | bytes 4718600 | tf_op jit(solution)/shard_map/ppermute | solution.py:16
  215.7 48.5 %copy-start.27 = (bf16[2,96,4096]{2,1,0:T(8,128)(2,1)S(1)}, bf16[2,96,4096]{2,1,0:T(8,128)(2,1)}, u32[]{:S(2)}) copy-start(bf16[2,96,4096]{2,1,0:T(8,128)(2,1)} %copy-done.26) | copy-start | bytes 4718596
  220.1 51.7 %copy-start.114 = (s32[1,2]{1,0:T(1,128)S(1)}, s32[1,2]{1,0:T(1,128)}, u32[]{:S(2)}) copy-start(s32[1,2]{1,0:T(1,128)} %param.9) | copy-start | bytes 28
  220.1 148.3 %all-reduce.42.cloned.1.call-start = ((), (), s32[]{:S(2)}) async-start(), calls=%async_computation.5 | async-start | bytes 3145728 | tf_op jit(solution)/shard_map/psum | solution.py:129
  267.3 37.2 %collective-permute-start.2 = (bf16[2,96,4096]{2,1,0:T(8,128)(2,1)}, bf16[2,96,4096]{2,1,0:T(8,128)(2,1)}, u32[]{:S(2)}, u32[]{:S(2)}) collective-permute-start(bf16[2,96,4096]{2,1,0:T(8,128)(2,1)} %fusion.33), channel_id=1, source_target_pairs={{0,8},{8,16},{16,24},{1,9},{9,17},{17,25},{2,10},{10,18},{18,26},{... | collective-permute-start | bytes 4718600 | tf_op jit(solution)/shard_map/ppermute | solution.py:16
  323.9 125.2 %all-gather.9.cloned.1.call-start = ((), (), s32[]{:S(2)}) async-start(), calls=%async_computation.6 | async-start | bytes 7864320 | tf_op jit(solution)/shard_map/all_gather | solution.py:155
  324.2 71.9 %copy-start.60 = (bf16[2,96,4,128]{3,1,2,0:T(8,128)(2,1)}, bf16[2,96,4,128]{3,1,2,0:T(8,128)(2,1)S(1)}, u32[]{:S(2)}) copy-start(bf16[2,96,4,128]{3,1,2,0:T(8,128)(2,1)S(1)} %pad_maximum_fusion) | copy-start | bytes 589828
  324.5 71.9 %copy-start.88 = (f32[2,4,96]{2,1,0:T(4,128)}, f32[2,4,96]{2,1,0:T(4,128)S(1)}, u32[]{:S(2)}) copy-start(f32[2,4,96]{2,1,0:T(4,128)S(1)} %get-tuple-element.178) | copy-start | bytes 9220
  324.7 71.8 %copy-start.103 = (f32[2,4,96]{2,1,0:T(4,128)}, f32[2,4,96]{2,1,0:T(4,128)S(1)}, u32[]{:S(2)}) copy-start(f32[2,4,96]{2,1,0:T(4,128)S(1)} %fusion.513) | copy-start | bytes 9220
  324.7 70.1 %copy-start.92 = (f32[2,4,96]{2,1,0:T(4,128)}, f32[2,4,96]{2,1,0:T(4,128)S(1)}, u32[]{:S(2)}) copy-start(f32[2,4,96]{2,1,0:T(4,128)S(1)} %multiply_divide_fusion) | copy-start | bytes 9220
  326.6 68.1 %copy-start.53 = (bf16[2,96,128,1]{2,1,3,0:T(8,128)(2,1)}, bf16[2,96,128,1]{2,1,3,0:T(8,128)(2,1)S(1)}, u32[]{:S(2)}) copy-start(bf16[2,96,128,1]{2,1,3,0:T(8,128)(2,1)S(1)} %fusion.144) | copy-start | bytes 147460
  368.4 22.5 %copy-start.5 = (bf16[1,512,4096]{2,1,0:T(8,128)(2,1)S(1)}, bf16[1,512,4096]{2,1,0:T(8,128)(2,1)}, u32[]{:S(2)}) copy-start(bf16[1,512,4096]{2,1,0:T(8,128)(2,1)} %param.15) | copy-start | bytes 12582916
  372.8 18.1 %copy-start.93 = (f32[2,96]{1,0:T(2,128)S(1)}, f32[2,96]{1,0:T(2,128)}, u32[]{:S(2)}) copy-start(f32[2,96]{1,0:T(2,128)} %get-tuple-element.119) | copy-start | bytes 2308
  402.5 155.9 %all-gather.11.cloned.1.call-start = ((), (), s32[]{:S(2)}) async-start(), calls=%async_computation.7 | async-start | bytes 7864320 | tf_op jit(solution)/shard_map/all_gather | solution.py:155
  457.3 42.6 %copy-start.6 = (bf16[1,512,4096]{2,1,0:T(8,128)(2,1)S(1)}, bf16[1,512,4096]{2,1,0:T(8,128)(2,1)}, u32[]{:S(2)}) copy-start(bf16[1,512,4096]{2,1,0:T(8,128)(2,1)} %param.15) | copy-start | bytes 12582916
  458.5 38.6 %collective-permute-start.3 = (bf16[2,96,4096]{2,1,0:T(8,128)(2,1)S(1)}, bf16[2,96,4096]{2,1,0:T(8,128)(2,1)S(1)}, u32[]{:S(2)}, u32[]{:S(2)}) collective-permute-start(bf16[2,96,4096]{2,1,0:T(8,128)(2,1)S(1)} %fusion.42), channel_id=1, source_target_pairs={{8,0},{16,8},{24,16},{9,1},{17,9},{25,17},{10,2},{18,10},{26,18},{... | collective-permute-start | bytes 4718600 | tf_op jit(solution)/shard_map/ppermute | solution.py:16
  512.8 154.6 %all-gather.13.cloned.1.call-start = ((), (), s32[]{:S(2)}) async-start(), calls=%async_computation.8 | async-start | bytes 7864320 | tf_op jit(solution)/shard_map/all_gather | solution.py:155
  566.3 42.7 %copy-start.7 = (bf16[1,512,4096]{2,1,0:T(8,128)(2,1)S(1)}, bf16[1,512,4096]{2,1,0:T(8,128)(2,1)}, u32[]{:S(2)}) copy-start(bf16[1,512,4096]{2,1,0:T(8,128)(2,1)} %param.15) | copy-start | bytes 12582916
  567.7 38.4 %collective-permute-start.4 = (bf16[2,96,4096]{2,1,0:T(8,128)(2,1)S(1)}, bf16[2,96,4096]{2,1,0:T(8,128)(2,1)S(1)}, u32[]{:S(2)}, u32[]{:S(2)}) collective-permute-start(bf16[2,96,4096]{2,1,0:T(8,128)(2,1)S(1)} %fusion.39), channel_id=1, source_target_pairs={{8,0},{16,8},{24,16},{9,1},{17,9},{25,17},{10,2},{18,10},{26,18},{... | collective-permute-start | bytes 4718600 | tf_op jit(solution)/shard_map/ppermute | solution.py:16
  677.9 54.0 %collective-permute-start.5 = (bf16[2,96,4096]{2,1,0:T(8,128)(2,1)}, bf16[2,96,4096]{2,1,0:T(8,128)(2,1)}, u32[]{:S(2)}, u32[]{:S(2)}) collective-permute-start(bf16[2,96,4096]{2,1,0:T(8,128)(2,1)} %fusion.41), channel_id=1, source_target_pairs={{8,0},{16,8},{24,16},{9,1},{17,9},{25,17},{10,2},{18,10},{26,18},{... | collective-permute-start | bytes 4718600 | tf_op jit(solution)/shard_map/ppermute | solution.py:16
  689.4 77.2 %all-to-all-start = ((bf16[192,2,2048]{2,0,1:T(8,128)(2,1)}), bf16[192,2,2048]{2,0,1:T(8,128)(2,1)}, u32[]{:S(2)}, u32[]{:S(2)}) async-start(bf16[192,2,2048]{2,0,1:T(8,128)(2,1)} %copy.95), calls=%async_computation | async-start | bytes 3145728 | tf_op jit(solution)/shard_map/all_to_all | solution.py:237
  766.7 45.9 %all-to-all-start.1 = ((bf16[192,2,2048]{2,0,1:T(8,128)(2,1)}), bf16[192,2,2048]{2,0,1:T(8,128)(2,1)}, u32[]{:S(2)}, u32[]{:S(2)}) async-start(bf16[192,2,2048]{2,0,1:T(8,128)(2,1)} %fusion.63), calls=%async_computation.1 | async-start | bytes 3145728 | tf_op jit(solution)/shard_map/all_to_all | solution.py:238
  (98 other events, 380.9 us)
Sparse Core Ops, SparseCore 0:
  27.8 45.5 all-reduce.35
  124.4 45.3 all-reduce.37
  220.3 43.9 all-reduce.39
  324.0 44.3 all-reduce.41
  402.6 46.3 all-gather.8
  512.9 45.4 all-gather.10
  621.9 45.4 all-gather.12
